TPU v7x, 128 devices: a whole 4x4x4 slice. The times are simulated.
128 devices in a mesh: seq: 32 (over z, x, core), mp: 4 (over y).
Axes of the slice: x: 4, y: 4, z: 4, core: 2. Of those that a mesh axis runs over, the one named last changes fastest.
Arguments:
- teacher_query: bfloat16 [5120, 8192], P('seq', 'mp'), may hold values from -37 to 37
- teacher_keys: bfloat16 [5120, 1024], P('seq', 'mp'), may hold values from -4 to 4
- teacher_values: bfloat16 [5120, 1024], P('seq', 'mp'), may hold values from -4 to 4
- teacher_docs: int32 [16], replicated, may hold values from 1 to 3840, 5120 in all
- student_query: bfloat16 [5120, 3584], P('seq', 'mp'), may hold values from -37 to 37
- student_keys: bfloat16 [5120, 512], P('seq', 'mp'), may hold values from -4 to 4
- student_values: bfloat16 [5120, 512], P('seq', 'mp'), may hold values from -4 to 4
- student_docs: int32 [16], replicated, may hold values from 1 to 3840, 5120 in all
- projector: bfloat16 [8192, 3584], P('mp'), may hold values from -0.125 to 0.125
- teacher_spans: int32 [32, 2, 128], P('seq'), may hold values from 0 to 159, as said below
- student_spans: int32 [32, 2, 128], P('seq'), may hold values from 0 to 159, as said below
Outputs:
- grad_query: bfloat16 [5120, 3584], P('seq', 'mp')
- grad_keys: bfloat16 [5120, 512], P('seq', 'mp')
- grad_values: bfloat16 [5120, 512], P('seq', 'mp')
Inputs may be any that keep to these rules, and one draw needn't show every extreme that they name: `teacher_spans`: column d * 4 + c of row r holds, first, the first teacher position of a span (counted within the 160 positions of index r along seq) and, second, its number of positions; it is the c-th span that index r sends to index d. A count of 0 marks an empty slot; the live slots of one destination come first; live spans cover 1 to 4 positions inside the index's positions and may intersect. One source sends at most 4 spans to one destination, and in every draw some destination receives 4 from every source. `student_spans`: column r * 4 + c of row d holds the student range (first position within the 160 positions of index d along seq, then the number of positions) of the span in column d * 4 + c of row r of teacher_spans; the count is 0 exactly where that teacher slot is empty, else 1 to 4. Ranges may intersect.
All inputs are finite; a program needn't handle non-finite values.
Results may differ from a plain program's by a relative error of at most 0.015.
Values may be sent and summed in bfloat16 or wider, within the bound.
A program may use at most 128 MiB of HBM per device.

v0:
```python
import jax
import jax.numpy as jnp
from jax import lax
from jax.sharding import PartitionSpec as P

HD = 128
NEG = -1e30


def sent_together(arrays, axis, dim, along):
    ends, at = ([], 0)
    for a in arrays[:-1]:
        at += a.shape[along]
        ends.append(at)
    both = jnp.concatenate(arrays, axis=along)
    return tuple(jnp.split(lax.all_gather(both, axis, axis=dim, tiled=True), ends, axis=along))


def doc_index(lengths, positions):
    bounds = jnp.cumsum(lengths)
    return jnp.sum((bounds[None, :] <= positions[:, None]).astype(jnp.int32), axis=1)


def block_size(total_rows):
    size_now = min(512, total_rows)
    while total_rows % size_now:
        size_now -= 1
    return size_now


def keep_same(carried):
    return carried


def allowed_pairs(query_docs, query_places, docs, key_places):
    same_doc = doc_index(docs, key_places)[None, :] == query_docs[:, None]
    return same_doc & (key_places[None, :] <= query_places[:, None])


def members(spans, tok_rows):
    starts = spans[0, 0]
    lengths = spans[0, 1]
    places = jnp.arange(tok_rows, dtype=jnp.int32)
    inside = (places[None, :] >= starts[:, None]) & (places[None, :] < (starts + lengths)[:, None])
    return (inside.astype(jnp.bfloat16), 1.0 / jnp.maximum(lengths, 1).astype(jnp.float32))


def empty_state(tok_rows, groups_here, head_ratio):
    return (
        jnp.full((groups_here, head_ratio, tok_rows), NEG, jnp.float32),
        jnp.zeros((groups_here, head_ratio, tok_rows), jnp.float32),
        jnp.zeros((groups_here, head_ratio, tok_rows, HD), jnp.float32),
    )


def attend_block(running, queries, key_block, value_block, allowed, score_scale):
    row_peak, totals, weighted = running
    scores = (
        jnp.einsum("qgrd,kgd->grqk", queries, key_block, preferred_element_type=jnp.float32)
        * score_scale
    )
    scores = jnp.where(allowed[None, None], scores, NEG)
    new_peak = jnp.maximum(row_peak, jnp.max(scores, axis=-1))
    weights = jnp.where(allowed[None, None], jnp.exp(scores - new_peak[..., None]), 0.0)
    factor = jnp.exp(row_peak - new_peak)
    totals = totals * factor + jnp.sum(weights, axis=-1)
    contrib = jnp.einsum(
        "grqk,kgd->grqd",
        weights.astype(jnp.bfloat16),
        value_block,
        preferred_element_type=jnp.float32,
    )
    return (new_peak, totals, weighted * factor[..., None] + contrib)


def fold_attention(running, queries, key_rows, value_rows, query_docs, query_places, docs):
    piece_rows = key_rows.shape[0]
    groups_here = queries.shape[1]
    step_rows = block_size(piece_rows)
    count_blocks = piece_rows // step_rows
    key_blocks = key_rows.reshape(count_blocks, step_rows, groups_here, HD)
    value_blocks = value_rows.reshape(count_blocks, step_rows, groups_here, HD)
    score_scale = HD ** (-0.5)

    def one_step(carried, inputs):
        number, key_block, value_block = inputs
        key_places = number * step_rows + jnp.arange(step_rows, dtype=jnp.int32)
        allowed = allowed_pairs(query_docs, query_places, docs, key_places)

        def compute(current):
            return attend_block(current, queries, key_block, value_block, allowed, score_scale)

        return (lax.cond(jnp.any(allowed), compute, keep_same, carried), None)

    result, unused = lax.scan(
        one_step, running, (jnp.arange(count_blocks, dtype=jnp.int32), key_blocks, value_blocks)
    )
    return result


def finish(running, tok_rows):
    row_peak, totals, weighted = (running[0], running[1], running[2])
    context = weighted / totals[..., None]
    context = jnp.transpose(context, (2, 0, 1, 3)).reshape(tok_rows, -1).astype(jnp.bfloat16)
    log_sums = jnp.transpose(row_peak + jnp.log(totals), (2, 0, 1)).reshape(tok_rows, -1)
    return (context, log_sums)


def backward_block(
    queries, douts, sums_here, deltas_here, key_block, value_block, allowed, score_scale
):
    scores = (
        jnp.einsum("qgrd,kgd->grqk", queries, key_block, preferred_element_type=jnp.float32)
        * score_scale
    )
    probs = jnp.where(allowed[None, None], jnp.exp(scores - sums_here[..., None]), 0.0)
    prob_grad = jnp.einsum("qgrd,kgd->grqk", douts, value_block, preferred_element_type=jnp.float32)
    dscore = (probs * (prob_grad - deltas_here[..., None])).astype(jnp.bfloat16)
    return (probs.astype(jnp.bfloat16), dscore)


def key_term(probs_low, dscore, queries, douts, score_scale):
    key_grad = (
        jnp.einsum("grqk,qgrd->kgd", dscore, queries, preferred_element_type=jnp.float32)
        * score_scale
    )
    value_grad = jnp.einsum("grqk,qgrd->kgd", probs_low, douts, preferred_element_type=jnp.float32)
    rows_here = key_grad.shape[0]
    return jnp.concatenate(
        [key_grad.reshape(rows_here, -1), value_grad.reshape(rows_here, -1)], axis=1
    )


def fold_grads(
    running,
    queries,
    douts,
    sums_here,
    deltas_here,
    query_docs,
    query_places,
    docs,
    key_rows,
    value_rows,
):
    piece_rows = key_rows.shape[0]
    groups_here = queries.shape[1]
    step_rows = block_size(piece_rows)
    count_blocks = piece_rows // step_rows
    key_blocks = key_rows.reshape(count_blocks, step_rows, groups_here, HD)
    value_blocks = value_rows.reshape(count_blocks, step_rows, groups_here, HD)
    score_scale = HD ** (-0.5)
    term_width = 2 * groups_here * HD

    def one_step(carried, inputs):
        number, key_block, value_block = inputs
        key_places = number * step_rows + jnp.arange(step_rows, dtype=jnp.int32)
        allowed = allowed_pairs(query_docs, query_places, docs, key_places)

        def compute(current):
            probs_low, dscore = backward_block(
                queries, douts, sums_here, deltas_here, key_block, value_block, allowed, score_scale
            )
            updated = (
                current
                + jnp.einsum(
                    "grqk,kgd->qgrd", dscore, key_block, preferred_element_type=jnp.float32
                )
                * score_scale
            )
            return (updated, key_term(probs_low, dscore, queries, douts, score_scale))

        def passing(current):
            return (current, jnp.zeros((step_rows, term_width), jnp.float32))

        return lax.cond(jnp.any(allowed), compute, passing, carried)

    grad_query, terms = lax.scan(
        one_step, running[0], (jnp.arange(count_blocks, dtype=jnp.int32), key_blocks, value_blocks)
    )
    key_terms = terms.reshape(piece_rows, term_width)
    return (grad_query, key_terms)


def body(
    teacher_query,
    teacher_keys,
    teacher_values,
    teacher_docs,
    student_query,
    student_keys,
    student_values,
    student_docs,
    projector,
    teacher_spans,
    student_spans,
):
    tok_rows = teacher_query.shape[0]
    all_rows = tok_rows * lax.axis_size("seq")
    teacher_groups = teacher_keys.shape[1] // HD
    teacher_ratio = teacher_query.shape[1] // HD // teacher_groups
    student_groups = student_keys.shape[1] // HD
    student_ratio = student_query.shape[1] // HD // student_groups
    query_places = lax.axis_index("seq") * tok_rows + jnp.arange(tok_rows, dtype=jnp.int32)
    teacher_qdocs = doc_index(teacher_docs, query_places)
    student_qdocs = doc_index(student_docs, query_places)
    teacher_q = teacher_query.reshape(tok_rows, teacher_groups, teacher_ratio, HD)
    student_q = student_query.reshape(tok_rows, student_groups, student_ratio, HD)
    teacher_init = empty_state(tok_rows, teacher_groups, teacher_ratio)
    student_init = empty_state(tok_rows, student_groups, student_ratio)
    pieces = (
        lax.all_gather(teacher_keys, "seq", axis=0, tiled=True),
        lax.all_gather(teacher_values, "seq", axis=0, tiled=True),
    )
    teacher_state = fold_attention(
        teacher_init, teacher_q, pieces[0], pieces[1], teacher_qdocs, query_places, teacher_docs
    )
    pieces = (
        lax.all_gather(student_keys, "seq", axis=0, tiled=True),
        lax.all_gather(student_values, "seq", axis=0, tiled=True),
    )
    attended = fold_attention(
        student_init[:3], student_q, pieces[0], pieces[1], student_qdocs, query_places, student_docs
    )
    student_state = tuple(attended)
    teacher_context, unused = finish(teacher_state, tok_rows)
    member_teacher, weight_teacher = members(teacher_spans, tok_rows)
    pooled_teacher = (
        jnp.dot(member_teacher, teacher_context, preferred_element_type=jnp.float32)
        * weight_teacher[:, None]
    ).astype(jnp.bfloat16)
    projected = jnp.dot(pooled_teacher, projector, preferred_element_type=jnp.float32)
    targets = lax.psum_scatter(
        projected.astype(jnp.bfloat16), "mp", scatter_dimension=1, tiled=True
    )
    arrived = lax.all_to_all(targets, "seq", split_axis=0, concat_axis=0, tiled=True)
    student_context, student_sums = finish(student_state, tok_rows)
    member_student, weight_student = members(student_spans, tok_rows)
    pooled_student = (
        jnp.dot(member_student, student_context, preferred_element_type=jnp.float32)
        * weight_student[:, None]
    )
    live_rows = (student_spans[0, 1] > 0)[:, None]
    residual = (
        jnp.where(live_rows, pooled_student - arrived.astype(jnp.float32), 0.0)
        * weight_student[:, None]
    )
    grad_out = jnp.dot(jnp.transpose(member_student.astype(jnp.float32)), residual).astype(
        jnp.bfloat16
    )
    heads_here = student_groups * student_ratio
    deltas = jnp.sum(
        (grad_out.astype(jnp.float32) * student_context.astype(jnp.float32)).reshape(
            tok_rows, heads_here, HD
        ),
        axis=-1,
    )
    student_dout = grad_out.reshape(tok_rows, student_groups, student_ratio, HD)
    sums_here = jnp.transpose(
        student_sums.reshape(tok_rows, student_groups, student_ratio), (1, 2, 0)
    )
    deltas_here = jnp.transpose(deltas.reshape(tok_rows, student_groups, student_ratio), (1, 2, 0))
    term_width = 2 * student_keys.shape[1]
    grad_init = (jnp.zeros((tok_rows, student_groups, student_ratio, HD), jnp.float32),)
    grad_init = grad_init + (jnp.zeros((all_rows, term_width), jnp.float32),)
    pieces = sent_together((student_keys, student_values), "seq", 0, 1)
    grad_state = fold_grads(
        grad_init,
        student_q,
        student_dout,
        sums_here,
        deltas_here,
        student_qdocs,
        query_places,
        student_docs,
        pieces[0],
        pieces[1],
    )
    grad_query = grad_state[0].reshape(tok_rows, -1).astype(jnp.bfloat16)
    key_terms = lax.psum_scatter(
        grad_state[1].astype(jnp.bfloat16), "seq", scatter_dimension=0, tiled=True
    ).astype(jnp.float32)
    half_width = student_keys.shape[1]
    return (
        grad_query,
        key_terms[:, :half_width].astype(jnp.bfloat16),
        key_terms[:, half_width:].astype(jnp.bfloat16),
    )


def solution(mesh):
    return jax.shard_map(
        body,
        mesh=mesh,
        in_specs=(
            P("seq", "mp"),
            P("seq", "mp"),
            P("seq", "mp"),
            P(),
            P("seq", "mp"),
            P("seq", "mp"),
            P("seq", "mp"),
            P(),
            P("mp", None),
            P("seq", None, None),
            P("seq", None, None),
        ),
        out_specs=(P("seq", "mp"), P("seq", "mp"), P("seq", "mp")),
        check_vma=False,
    )
```

profile of v0, /device:TPU:0, one launch (start us, length us, event | category | flops | bytes accessed | tf_op | source)
XLA Modules:
  0.0 442.9 jit_solution(18287715508610465166)
XLA Ops:
  13.8 1.2 copy.55
  15.3 41.9 %all-gather.12.cloned.1.call-done = bf16[5120,256]{1,0:T(8,128)(2,1)} async-done(((bf16[160,256]{1,0:T(8,128)(2,1)}), bf16[5120,256]{1,0:T(8,128)(2,1)}) %all-gather.12.cloned.1.call-update) | async-done | bytes 2621456 | tf_op jit(solution)/shard_map/all_gather | solution.py:212
  57.2 3.5 reshape.307
  60.8 2.1 copy.41
  62.8 40.4 %all-gather.14.cloned.1.call-done = bf16[5120,256]{1,0:T(8,128)(2,1)} async-done(((bf16[160,256]{1,0:T(8,128)(2,1)}), bf16[5120,256]{1,0:T(8,128)(2,1)}) %all-gather.14.cloned.1.call-update) | async-done | bytes 2621456 | tf_op jit(solution)/shard_map/all_gather | solution.py:213
  103.2 3.5 reshape.309
  106.8 2.0 copy.43
  109.0 35.1 %while.53 = (s32[]{:T(128)}, f32[2,8,160]{2,1,0:T(8,128)S(1)}, f32[2,8,160]{2,1,0:T(8,128)S(1)}, f32[2,8,160,128]{3,2,1,0:T(8,128)S(1)}, s32[1,16]{1,0:T(1,128)S...) while((s32[]{:T(128)}, f32[2,8,160]{2,1,0:T(8,128)S(1)}, ...), condition=%wide.region_19.20_spmd.clone, body=%wide.region_12.19_spmd.clone.sunk | while | flops 689140928 | bytes 20034780 | solution.py:95
  111.8 7.0 %conditional.10 = ((f32[2,8,160]{2,1,0:T(8,128)S(1)}, f32[2,8,160]{2,1,0:T(8,128)S(1)}, f32[2,8,160,128]{3,2,1,0:T(8,128)S(1)})) conditional(s32[]{:T(128)} %convert_element_type.203, (f32[2,8,160]{2,1,0:T(8,128)S(1)}, f32[2,8,160]{2,1,0:T(8,128)S(1)}, f32[2,8,160,128]{3,2,1,0:T(8,128)S(1)}) %tuple.156, (pred[160,512]{1,0:T(8,128)(4,1)S(1)}, ...), branch_computations={%region_15.15_spmd, %region_16.18_spmd} | conditional | flops 688788480 | bytes 19940384 | solution.py:93
  111.8 2.0 fusion.29
  113.8 1.9 fusion.31
  115.7 3.1 fusion.35
  144.7 7.5 %convolution_convert_fusion = bf16[128,3584]{1,0:T(8,128)(2,1)S(1)} fusion(bf16[2048,3584]{1,0:T(8,128)(2,1)} %param.31, bf16[20,8,16,128]{3,2,1,0:T(8,128)(2,1)S(1)} %bitcast.238, f32[128]{0:T(128)S(1)} %fusion.114, s32[128]{0:T(128)S(1)} %bitcast_add_fusion.1, s32[128]{0:T(128)S(1)} %slice_bitcast_fusion), kind=kOutput, calls=%fused_computation.100 | convolution fusion | flops 1963978752 | bytes 16254464 | tf_op jit(solution)/shard_map/dot_general | solution.py:232
  152.2 1.3 copy.52
  155.0 36.9 %all-gather.10.cloned.1.call-done = bf16[5120,128]{1,0:T(8,128)(2,1)} async-done(((bf16[160,128]{1,0:T(8,128)(2,1)}), bf16[5120,128]{1,0:T(8,128)(2,1)}) %all-gather.10.cloned.1.call-update) | async-done | bytes 1310736 | tf_op jit(solution)/shard_map/all_gather | solution.py:220
  192.0 32.4 %while.52 = (s32[]{:T(128)}, f32[1,7,160]{2,1,0:T(8,128)S(1)}, f32[1,7,160]{2,1,0:T(8,128)S(1)}, f32[1,7,160,128]{3,2,1,0:T(8,128)S(1)}, s32[1,16]{1,0:T(1,128)S...) while((s32[]{:T(128)}, f32[1,7,160]{2,1,0:T(8,128)S(1)}, ...), condition=%wide.region_9.10_spmd.clone, body=%wide.region_2.9_spmd.clone.sunk | while | flops 301698496 | bytes 8989915 | solution.py:95
  194.8 4.3 conditional.9
  194.8 1.5 fusion.6
  196.3 1.9 fusion.9
  198.2 0.9 fusion.8
  224.8 5.7 %reduce-scatter.7.cloned.1.call-done = bf16[896,128]{1,0:T(8,128)(2,1)} async-done(((bf16[3584,128]{1,0:T(8,128)(2,1)}), bf16[896,128]{1,0:T(8,128)(2,1)}) %reduce-scatter.7.cloned.1.call-update) | async-done | bytes 229392
  230.5 1.1 copy.53
  232.3 42.8 %all-to-all-start = ((bf16[32,4,896]{2,1,0:T(4,128)(2,1)}), bf16[32,4,896]{2,1,0:T(4,128)(2,1)S(1)}, u32[]{:S(2)}, u32[]{:S(2)}) async-start(bf16[32,4,896]{2,1,0:T(4,128)(2,1)} %all_to_all.6), calls=%async_computation | async-start | bytes 458752 | tf_op jit(solution)/shard_map/all_to_all | solution.py:236
  275.2 1.6 all-gather.6.cloned.1.call-done
  276.8 3.0 fusion.121
  279.8 3.8 all-to-all-done
  285.0 39.6 %while.54 = (s32[]{:T(128)}, f32[160,1,7,128]{3,0,2,1:T(8,128)S(1)}, bf16[10,512,256]{1,2,0:T(8,128)(2,1)}, s32[1,16]{1,0:T(1,128)S(1)}, s32[10]{0:T(128)S(1)}, ...) while((s32[]{:T(128)}, ...), condition=%wide.region_27.28_spmd.clone, body=%wide.region_22.27_spmd.clone.sunk | while | flops 741032128 | bytes 14592339 | solution.py:178
  287.8 4.0 conditional.11
  288.3 1.8 fusion.53
  324.5 4.4 copy.49
  329.9 104.8 %reduce-scatter.5.cloned.1.call-done = bf16[160,256]{1,0:T(8,128)(2,1)} async-done(((bf16[5120,256]{1,0:T(8,128)(2,1)}), bf16[160,256]{1,0:T(8,128)(2,1)}) %reduce-scatter.5.cloned.1.call-update) | async-done | bytes 81936 | tf_op jit(solution)/shard_map/reduce_scatter | solution.py:280
  434.6 1.4 fusion.122
  (272 shorter events, 66.7 us)
Async XLA Ops:
  7.2 50.0 %all-gather.12.cloned.1.call-start = ((), (), s32[]{:S(2)}) async-start(), calls=%async_computation.6 | async-start | bytes 2703360 | tf_op jit(solution)/shard_map/all_gather | solution.py:212
  7.9 95.3 %all-gather.14.cloned.1.call-start = ((), (), s32[]{:S(2)}) async-start(), calls=%async_computation.7 | async-start | bytes 2703360 | tf_op jit(solution)/shard_map/all_gather | solution.py:213
  8.6 146.3 %all-gather.8.cloned.1.call-start = ((), (), s32[]{:S(2)}) async-start(), calls=%async_computation.4 | async-start | bytes 1351680 | tf_op jit(solution)/shard_map/all_gather | solution.py:219
  9.4 182.5 %all-gather.10.cloned.1.call-start = ((), (), s32[]{:S(2)}) async-start(), calls=%async_computation.5 | async-start | bytes 1351680 | tf_op jit(solution)/shard_map/all_gather | solution.py:220
  10.0 220.5 %reduce-scatter.7.cloned.1.call-start = ((), (), s32[]{:S(2)}) async-start(), calls=%async_computation.9 | async-start | bytes 1146880
  152.2 1.6 copy-start.1
  152.2 1.6 copy-start.2
  152.2 2.3 copy-start.3
  152.2 2.3 copy-start
  153.6 123.2 %all-gather.6.cloned.1.call-start = ((), (), s32[]{:S(2)}) async-start(), calls=%async_computation.3 | async-start | bytes 2703360 | tf_op jit(solution)/shard_map/all_gather | solution.py:16
  232.3 51.3 %all-to-all-start = ((bf16[32,4,896]{2,1,0:T(4,128)(2,1)}), bf16[32,4,896]{2,1,0:T(4,128)(2,1)S(1)}, u32[]{:S(2)}, u32[]{:S(2)}) async-start(bf16[32,4,896]{2,1,0:T(4,128)(2,1)} %all_to_all.6), calls=%async_computation | async-start | bytes 458752 | tf_op jit(solution)/shard_map/all_to_all | solution.py:236
  275.2 159.5 %reduce-scatter.5.cloned.1.call-start = ((), (), s32[]{:S(2)}) async-start(), calls=%async_computation.8 | async-start | bytes 2703360 | tf_op jit(solution)/shard_map/reduce_scatter | solution.py:280
Sparse Core Ops, SparseCore 0:
  10.2 46.9 all-gather.11
  59.5 43.7 all-gather.13
  105.5 42.1 all-gather.7
  149.8 42.1 all-gather.9
  194.2 36.2 reduce-scatter.6
  232.6 44.1 all-gather.5
  329.1 105.5 reduce-scatter.4
where the time goes:
time: 445 us; the launch traced here: 443 us
  waiting for transfers between devices  238 us (53%)
  local copies, waits for them, and re-layouts  52.7 us (12%)
  starting transfers between devices  43.3 us (10%)
  loops' own time  40.6 us (9%)
  other arithmetic  33.8 us (8%)
  matrix products  20.3 us (5%)
  between operations  14.5 us (3%)
    reduce_scatter x1, waiting for transfers between devices, body(): lax.psum_scatter(grad_state[1].astype(jnp.bfloat16), 'seq', scatter_dimen...  105 us
    all_to_all x1, starting transfers between devices, body(): lax.all_to_all(targets, 'seq', split_axis=0, concat_axis=0, tiled=True)  42.8 us
    all_gather x1, waiting for transfers between devices, body(): lax.all_gather(teacher_keys, 'seq', axis=0, tiled=True)  41.9 us
    all_gather x1, waiting for transfers between devices, body(): lax.all_gather(teacher_values, 'seq', axis=0, tiled=True)  40.4 us
    all_gather x1, waiting for transfers between devices, body(): lax.all_gather(student_values, 'seq', axis=0, tiled=True)  36.9 us
    another operation x2, loops' own time, fold_attention(): lax.scan(one_step, running, (jnp.arange(count_blocks, dtype=jnp.int32), k...  26.8 us
    dynamic_slice x30, local copies, waits for them, and re-layouts, fold_attention(): lax.scan(one_step, running, (jnp.arange(count_blocks, dtype=jnp.int32), k...  17.6 us
    reduce_or x20, other arithmetic, one_step(): return (lax.cond(jnp.any(allowed), compute, keep_same, carried), None)  15.6 us
  transfers between devices with their start and end apart: 8, of which 7 were waited for; matrix products, arithmetic and copies ran while one was open for 16% of the time, Pallas kernels for 0%

commit v1 on v0

--- a/solution.py
+++ b/solution.py
@@ -215,9 +215,18 @@
     teacher_state = fold_attention(
         teacher_init, teacher_q, pieces[0], pieces[1], teacher_qdocs, query_places, teacher_docs
     )
+
+    def resolve_the_figure(local_array, on_dim):
+        return jnp.concatenate(
+            lax.all_to_all(
+                jnp.stack(tuple((local_array for _ in range(lax.axis_size("seq"))))), "seq", 0, 0
+            ),
+            axis=on_dim,
+        )
+
     pieces = (
         lax.all_gather(student_keys, "seq", axis=0, tiled=True),
-        lax.all_gather(student_values, "seq", axis=0, tiled=True),
+        resolve_the_figure(student_values, 0),
     )
     attended = fold_attention(
         student_init[:3], student_q, pieces[0], pieces[1], student_qdocs, query_places, student_docs

time: 445 us -> 466 us (1.047)
  starting transfers between devices: 43.3 us -> 87 us
  waiting for transfers between devices: 238 us -> 214 us
    all_to_all x0 -> x1, starting transfers between devices: none -> 59.7 us  [resolve_the_figure(): lax.all_to_all(jnp.stack(tuple((local_array for _ in range(lax.axis_size(...]
    all_gather x1 -> x0, waiting for transfers between devices: 36.9 us -> none  [body(): lax.all_gather(student_values, 'seq', axis=0, tiled=True)]
    all_to_all x0 -> x1, waiting for transfers between devices: none -> 19.2 us  [resolve_the_figure(): lax.all_to_all(jnp.stack(tuple((local_array for _ in range(lax.axis_size(...]
    all_to_all x1, starting transfers between devices: 42.8 us -> 27 us  [body(): lax.all_to_all(targets, 'seq', split_axis=0, concat_axis=0, tiled=True)]
    unnamed x8 -> x7, waiting for transfers between devices: 8.29 us -> 2.13 us
  transfers between devices with their start and end apart: 8 -> 8, of which waited for: 7 -> 5; matrix products, arithmetic and copies ran while one was open for 16% -> 16% of each run, Pallas kernels for 0% -> 0%
where the time goes in v1:
time: 466 us; the launch traced here: 464 us
  waiting for transfers between devices  214 us (46%)
  starting transfers between devices  87 us (19%)
  local copies, waits for them, and re-layouts  54 us (12%)
  loops' own time  40.6 us (9%)
  other arithmetic  33.8 us (7%)
  matrix products  19.5 us (4%)
  between operations  14.5 us (3%)
    reduce_scatter x1, waiting for transfers between devices, body(): lax.psum_scatter(grad_state[1].astype(jnp.bfloat16), 'seq', scatter_dimen...  105 us
    all_to_all x1, starting transfers between devices, resolve_the_figure(): lax.all_to_all(jnp.stack(tuple((local_array for _ in range(lax.axis_size(...  59.7 us
    all_gather x1, waiting for transfers between devices, body(): lax.all_gather(teacher_keys, 'seq', axis=0, tiled=True)  42.5 us
    all_gather x1, waiting for transfers between devices, body(): lax.all_gather(teacher_values, 'seq', axis=0, tiled=True)  40.4 us
    all_to_all x1, starting transfers between devices, body(): lax.all_to_all(targets, 'seq', split_axis=0, concat_axis=0, tiled=True)  27 us
    another operation x2, loops' own time, fold_attention(): lax.scan(one_step, running, (jnp.arange(count_blocks, dtype=jnp.int32), k...  26.7 us
    all_to_all x1, waiting for transfers between devices, resolve_the_figure(): lax.all_to_all(jnp.stack(tuple((local_array for _ in range(lax.axis_size(...  19.2 us
    dynamic_slice x30, local copies, waits for them, and re-layouts, fold_attention(): lax.scan(one_step, running, (jnp.arange(count_blocks, dtype=jnp.int32), k...  17.6 us
  transfers between devices with their start and end apart: 8, of which 5 were waited for; matrix products, arithmetic and copies ran while one was open for 16% of the time, Pallas kernels for 0%

profile of v1, /device:TPU:0, one launch (start us, length us, event | category | flops | bytes accessed | tf_op | source)
XLA Modules:
  0.0 463.6 jit_solution(7219880477021088736)
XLA Ops:
  13.2 1.2 copy.55
  14.7 42.5 %all-gather.9.cloned.1.call-done = bf16[5120,256]{1,0:T(8,128)(2,1)} async-done(((bf16[160,256]{1,0:T(8,128)(2,1)}), bf16[5120,256]{1,0:T(8,128)(2,1)}) %all-gather.9.cloned.1.call-update) | async-done | bytes 2621456 | tf_op jit(solution)/shard_map/all_gather | solution.py:212
  57.2 3.5 reshape.305
  60.8 2.1 copy.41
  62.8 40.4 %all-gather.11.cloned.1.call-done = bf16[5120,256]{1,0:T(8,128)(2,1)} async-done(((bf16[160,256]{1,0:T(8,128)(2,1)}), bf16[5120,256]{1,0:T(8,128)(2,1)}) %all-gather.11.cloned.1.call-update) | async-done | bytes 2621456 | tf_op jit(solution)/shard_map/all_gather | solution.py:213
  103.2 3.5 reshape.307
  106.8 2.0 copy.43
  109.0 35.1 %while.53 = (s32[]{:T(128)}, f32[2,8,160]{2,1,0:T(8,128)S(1)}, f32[2,8,160]{2,1,0:T(8,128)S(1)}, f32[2,8,160,128]{3,2,1,0:T(8,128)S(1)}, s32[1,16]{1,0:T(1,128)S...) while((s32[]{:T(128)}, f32[2,8,160]{2,1,0:T(8,128)S(1)}, ...), condition=%wide.region_19.20_spmd.clone, body=%wide.region_12.19_spmd.clone.sunk | while | flops 689140928 | bytes 20034780 | solution.py:95
  111.8 7.0 %conditional.10 = ((f32[2,8,160]{2,1,0:T(8,128)S(1)}, f32[2,8,160]{2,1,0:T(8,128)S(1)}, f32[2,8,160,128]{3,2,1,0:T(8,128)S(1)})) conditional(s32[]{:T(128)} %convert_element_type.203, (f32[2,8,160]{2,1,0:T(8,128)S(1)}, f32[2,8,160]{2,1,0:T(8,128)S(1)}, f32[2,8,160,128]{3,2,1,0:T(8,128)S(1)}) %tuple.156, (pred[160,512]{1,0:T(8,128)(4,1)S(1)}, ...), branch_computations={%region_15.15_spmd, %region_16.18_spmd} | conditional | flops 688788480 | bytes 19940384 | solution.py:93
  111.8 2.0 fusion.29
  113.8 1.9 fusion.31
  115.7 3.1 fusion.35
  144.7 7.5 %convolution_convert_fusion = bf16[128,3584]{1,0:T(8,128)(2,1)S(1)} fusion(bf16[2048,3584]{1,0:T(8,128)(2,1)} %param.31, bf16[20,8,16,128]{3,2,1,0:T(8,128)(2,1)S(1)} %bitcast.238, f32[128]{0:T(128)S(1)} %fusion.114, s32[128]{0:T(128)S(1)} %bitcast_add_fusion.1, s32[128]{0:T(128)S(1)} %slice_bitcast_fusion), kind=kOutput, calls=%fused_computation.100 | convolution fusion | flops 1963978752 | bytes 16254464 | tf_op jit(solution)/shard_map/dot_general | solution.py:241
  152.2 1.3 copy.52
  153.6 1.2 stack.2
  154.8 59.7 %all-to-all-start = ((bf16[32,160,128]{2,1,0:T(8,128)(2,1)}), bf16[32,160,128]{2,1,0:T(8,128)(2,1)S(1)}, u32[]{:S(2)}, u32[]{:S(2)}) async-start(bf16[32,160,128]{2,1,0:T(8,128)(2,1)} %stack.2), calls=%async_computation | async-start | bytes 2621440 | tf_op jit(solution)/shard_map/all_to_all | solution.py:221
  215.8 19.2 %all-to-all-done = bf16[32,160,128]{2,1,0:T(8,128)(2,1)S(1)} async-done(((bf16[32,160,128]{2,1,0:T(8,128)(2,1)}), bf16[32,160,128]{2,1,0:T(8,128)(2,1)S(1)}, u32[]{:S(2)}, u32[]{:S(2)}) %all-to-all-start) | async-done | bytes 1310752 | tf_op jit(solution)/shard_map/all_to_all | solution.py:221
  235.1 31.5 %while.52 = (s32[]{:T(128)}, f32[1,7,160]{2,1,0:T(8,128)S(1)}, f32[1,7,160]{2,1,0:T(8,128)S(1)}, f32[1,7,160,128]{3,2,1,0:T(8,128)S(1)}, s32[1,16]{1,0:T(1,128)S...) while((s32[]{:T(128)}, f32[1,7,160]{2,1,0:T(8,128)S(1)}, ...), condition=%wide.region_9.10_spmd.clone, body=%wide.region_2.9_spmd.clone.sunk | while | flops 301698496 | bytes 8996831 | solution.py:95
  237.9 3.4 conditional.9
  237.9 1.5 fusion.6
  239.4 1.0 fusion.9
  240.4 0.9 fusion.8
  267.0 1.1 copy.53
  268.9 27.0 %all-to-all-start.1 = ((bf16[32,4,896]{2,1,0:T(4,128)(2,1)}), bf16[32,4,896]{2,1,0:T(4,128)(2,1)S(1)}, u32[]{:S(2)}, u32[]{:S(2)}) async-start(bf16[32,4,896]{2,1,0:T(4,128)(2,1)} %all_to_all.10), calls=%async_computation.1 | async-start | bytes 458752 | tf_op jit(solution)/shard_map/all_to_all | solution.py:245
  296.0 3.0 fusion.121
  299.0 5.4 %all-to-all-done.1 = bf16[32,4,896]{2,1,0:T(4,128)(2,1)S(1)} async-done(((bf16[32,4,896]{2,1,0:T(4,128)(2,1)}), bf16[32,4,896]{2,1,0:T(4,128)(2,1)S(1)}, u32[]{:S(2)}, u32[]{:S(2)}) %all-to-all-start.1) | async-done | bytes 229408 | tf_op jit(solution)/shard_map/all_to_all | solution.py:245
  305.7 39.6 %while.54 = (s32[]{:T(128)}, f32[160,1,7,128]{3,0,2,1:T(8,128)S(1)}, bf16[10,512,256]{1,2,0:T(8,128)(2,1)}, s32[1,16]{1,0:T(1,128)S(1)}, s32[10]{0:T(128)S(1)}, ...) while((s32[]{:T(128)}, ...), condition=%wide.region_27.28_spmd.clone, body=%wide.region_22.27_spmd.clone.sunk | while | flops 741032128 | bytes 14592339 | solution.py:178
  308.5 4.0 conditional.11
  309.0 1.8 fusion.53
  345.3 4.4 copy.49
  350.7 104.7 %reduce-scatter.5.cloned.1.call-done = bf16[160,256]{1,0:T(8,128)(2,1)} async-done(((bf16[5120,256]{1,0:T(8,128)(2,1)}), bf16[160,256]{1,0:T(8,128)(2,1)}) %reduce-scatter.5.cloned.1.call-update) | async-done | bytes 81936 | tf_op jit(solution)/shard_map/reduce_scatter | solution.py:289
  455.3 1.4 fusion.122
  (272 shorter events, 66.1 us)
Async XLA Ops:
  7.2 50.0 %all-gather.9.cloned.1.call-start = ((), (), s32[]{:S(2)}) async-start(), calls=%async_computation.6 | async-start | bytes 2703360 | tf_op jit(solution)/shard_map/all_gather | solution.py:212
  7.9 95.3 %all-gather.11.cloned.1.call-start = ((), (), s32[]{:S(2)}) async-start(), calls=%async_computation.7 | async-start | bytes 2703360 | tf_op jit(solution)/shard_map/all_gather | solution.py:213
  8.6 226.4 %all-gather.7.cloned.1.call-start = ((), (), s32[]{:S(2)}) async-start(), calls=%async_computation.5 | async-start | bytes 1351680 | tf_op jit(solution)/shard_map/all_gather | solution.py:228
  9.4 257.7 %reduce-scatter.7.cloned.1.call-start = ((), (), s32[]{:S(2)}) async-start(), calls=%async_computation.9 | async-start | bytes 1146880
  152.2 1.4 copy-start.2
  153.5 61.2 %copy-start.1 = (bf16[160,128]{1,0:T(8,128)(2,1)S(1)}, bf16[160,128]{1,0:T(8,128)(2,1)}, u32[]{:S(2)}) copy-start(bf16[160,128]{1,0:T(8,128)(2,1)} %param.28) | copy-start | bytes 122884
  153.6 61.8 %copy-start = (bf16[160,896]{1,0:T(8,128)(2,1)S(1)}, bf16[160,896]{1,0:T(8,128)(2,1)}, u32[]{:S(2)}) copy-start(bf16[160,896]{1,0:T(8,128)(2,1)} %param.27) | copy-start | bytes 860164
  154.8 61.0 %copy-start.3 = (s32[1,2,128]{2,1,0:T(2,128)S(1)}, s32[1,2,128]{2,1,0:T(2,128)}, u32[]{:S(2)}) copy-start(s32[1,2,128]{2,1,0:T(2,128)} %param.33) | copy-start | bytes 3076
  154.8 80.2 %all-to-all-start = ((bf16[32,160,128]{2,1,0:T(8,128)(2,1)}), bf16[32,160,128]{2,1,0:T(8,128)(2,1)S(1)}, u32[]{:S(2)}, u32[]{:S(2)}) async-start(bf16[32,160,128]{2,1,0:T(8,128)(2,1)} %stack.2), calls=%async_computation | async-start | bytes 2621440 | tf_op jit(solution)/shard_map/all_to_all | solution.py:221
  214.5 81.5 %all-gather.5.cloned.1.call-start = ((), (), s32[]{:S(2)}) async-start(), calls=%async_computation.4 | async-start | bytes 2703360 | tf_op jit(solution)/shard_map/all_gather | solution.py:16
  268.9 35.4 %all-to-all-start.1 = ((bf16[32,4,896]{2,1,0:T(4,128)(2,1)}), bf16[32,4,896]{2,1,0:T(4,128)(2,1)S(1)}, u32[]{:S(2)}, u32[]{:S(2)}) async-start(bf16[32,4,896]{2,1,0:T(4,128)(2,1)} %all_to_all.10), calls=%async_computation.1 | async-start | bytes 458752 | tf_op jit(solution)/shard_map/all_to_all | solution.py:245
  295.9 159.4 %reduce-scatter.5.cloned.1.call-start = ((), (), s32[]{:S(2)}) async-start(), calls=%async_computation.8 | async-start | bytes 2703360 | tf_op jit(solution)/shard_map/reduce_scatter | solution.py:289
Sparse Core Ops, SparseCore 0:
  10.2 46.9 all-gather.8
  59.5 43.7 all-gather.10
  105.5 42.1 all-gather.6
  153.7 76.7 reduce-scatter.6
  232.5 44.2 all-gather.4
  349.8 105.4 reduce-scatter.4
